TPU v7x, 32 devices: a whole 2x2x4 slice. The times are simulated.
32 devices in a mesh: group: 2 (over y), ctx: 4 (over z), head: 4 (over x, core).
Axes of the slice: x: 2, y: 2, z: 4, core: 2. Of those that a mesh axis runs over, the one named last changes fastest.
Arguments:
- query_nope: bfloat16 [512, 8192], P(('group', 'ctx'), 'head'), parts along dimension 0, may hold values from -6 to 6
- query_rope: bfloat16 [512, 4096], P(('group', 'ctx'), 'head'), parts along dimension 0, may hold values from -16 to 16
- kv_latent: bfloat16 [512, 512], P(('group', 'ctx'), 'head'), parts along dimension 0, may hold values from -1300 to 1300
- key_rope: bfloat16 [512, 64], P(('group', 'ctx')), parts along dimension 0, may hold values from -16 to 16
- latent_gain: float32 [512], replicated, may hold values from 0.1 to 1.9
- w_key: bfloat16 [512, 8192], P(None, 'head'), may hold values from -0.25 to 0.25
- w_value: bfloat16 [512, 8192], P(None, 'head'), may hold values from -0.25 to 0.25
- block_order: int32 [16], P('group'), parts along dimension 0, may hold values from 0 to 7, as said below
Outputs:
- attention_out: bfloat16 [512, 8192], P(('group', 'ctx'), 'head'), parts along dimension 0
There are 2 independent parts, one for each index of `group`. A program takes and returns all parts, laid end to end along the dimension named above; an argument that names none is the same for every part. Nothing has to cross between parts.
Inputs may be any that keep to these rules, and one draw needn't show every extreme that they name: `block_order`: A permutation of 0 to 7. Entries 2 c and 2 c + 1, for each c < 4, add up to 7.
All inputs are finite; a program needn't handle non-finite values.
Results may differ from a plain program's by a relative error of at most 0.0081.
Values may be sent and summed in bfloat16 or wider, within the bound.
A program may use at most 64 MiB of HBM per device.

v0:
```python
from functools import partial
import math
import jax
import jax.numpy as jnp
from jax import lax
from jax.sharding import PartitionSpec as P

ROPE = 64
NOPE = 128
VALUE_DIM = 128
EPSILON = 1e-06
NEGATIVE = -1e30


def rope_angle(positions, width):
    half_width = width // 2
    frequency = jnp.exp(-jnp.log(10000.0) * jnp.arange(half_width, dtype=jnp.float32) / half_width)
    return positions.astype(jnp.float32)[:, None] * frequency[None, :]


def rotate_pairs(values, angle):
    half_width = values.shape[-1] // 2
    first_half = values[..., :half_width]
    second = values[..., half_width:]
    cosine = jnp.cos(angle)
    sine_part = jnp.sin(angle)
    return jnp.concatenate(
        [first_half * cosine - second * sine_part, second * cosine + first_half * sine_part], -1
    )


def block_positions(begin_row, row_count, table, block_rows):
    row_ids = begin_row + jnp.arange(row_count, dtype=jnp.int32)
    blocks = row_ids // block_rows
    slot_ids = jnp.arange(table.shape[0], dtype=jnp.int32)
    looked = jnp.sum(jnp.where(blocks[:, None] == slot_ids[None, :], table[None, :], 0), axis=1)
    return looked * block_rows + row_ids % block_rows


def block_length(row_count, shard_rows):
    best_rows = shard_rows
    for factor in range(1, row_count // shard_rows + 1):
        if row_count // shard_rows % factor == 0 and shard_rows * factor <= max(512, shard_rows):
            best_rows = shard_rows * factor
    return best_rows


def attend_block(
    carried,
    query_latent,
    query_rotated,
    query_place,
    key_latent,
    key_rotated,
    key_place,
    score_scale,
):
    running_max, running_total, summed = carried
    contract = (((1,), (1,)), ((), ()))
    scores = lax.dot_general(query_latent, key_latent, contract, preferred_element_type=jnp.float32)
    scores = (
        scores
        + lax.dot_general(query_rotated, key_rotated, contract, preferred_element_type=jnp.float32)
    ) * score_scale
    visible = key_place[None, :] <= query_place[:, None]
    scores = jnp.where(visible, scores, NEGATIVE)
    new_max = jnp.maximum(running_max, jnp.max(scores, axis=1))
    exps = jnp.where(visible, jnp.exp(scores - new_max[:, None]), 0.0)
    shrink = jnp.exp(running_max - new_max)
    running_total = running_total * shrink + jnp.sum(exps, axis=1)
    summed = summed * shrink[:, None] + jnp.dot(
        exps.astype(jnp.bfloat16), key_latent, preferred_element_type=jnp.float32
    )
    return (new_max, running_total, summed)


def per_device(
    query_nope, query_rope, kv_latent, key_rope, latent_gain, w_key, w_value, block_order
):
    tokens_here = query_nope.shape[0]
    heads_here = w_key.shape[1] // NOPE
    latent_width = w_key.shape[0]
    block_rows = tokens_here // 2
    score_scale = 1.0 / math.sqrt(NOPE + ROPE)
    first_row = lax.axis_index("ctx") * tokens_here
    query_place = block_positions(first_row, tokens_here, block_order, block_rows)
    query_angle = rope_angle(query_place, ROPE)
    query_rotated = rotate_pairs(
        query_rope.astype(jnp.float32).reshape(tokens_here, heads_here, ROPE),
        query_angle[:, None, :],
    )
    query_rotated = query_rotated.astype(jnp.bfloat16).reshape(tokens_here * heads_here, ROPE)
    absorbed = jnp.einsum(
        "thd,lhd->thl",
        query_nope.reshape(tokens_here, heads_here, NOPE),
        w_key.reshape(latent_width, heads_here, NOPE),
        preferred_element_type=jnp.float32,
    )
    absorbed = absorbed.astype(jnp.bfloat16).reshape(tokens_here * heads_here, latent_width)
    row_place = jnp.repeat(query_place, heads_here)
    groups = ((absorbed, query_rotated, row_place),)
    initial = tuple(
        (
            (
                jnp.full((member[0].shape[0],), NEGATIVE, jnp.float32),
                jnp.zeros((member[0].shape[0],), jnp.float32),
                jnp.zeros((member[0].shape[0], latent_width), jnp.float32),
            )
            for member in groups
        )
    )
    columns = kv_latent.shape[1]
    column_part = kv_latent.astype(jnp.float32)
    square = lax.psum(jnp.sum(column_part * column_part, axis=1), "head")
    gain_part = lax.dynamic_slice_in_dim(latent_gain, lax.axis_index("head") * columns, columns, 0)
    scaled = (
        column_part * lax.rsqrt(square / latent_width + EPSILON)[:, None] * gain_part[None, :]
    ).astype(jnp.bfloat16)
    normed = lax.all_gather(scaled, "head", axis=1, tiled=True)
    key_rotated = rotate_pairs(key_rope.astype(jnp.float32), query_angle).astype(jnp.bfloat16)
    key_latent = lax.all_gather(normed, "ctx", axis=0, tiled=True)
    make_key_rotated = lax.all_gather(key_rotated, "ctx", axis=0, tiled=True)
    row_count = key_latent.shape[0]
    length = block_length(row_count, tokens_here)
    block_count = row_count // length
    latent_blocks = key_latent.reshape(block_count, length, latent_width)
    rotated_blocks = make_key_rotated.reshape(block_count, length, ROPE)
    block_starts = length * jnp.arange(block_count, dtype=jnp.int32)

    def one_block(state_now, operands):
        latent_block, rotated_block, first_key = operands
        key_place = block_positions(first_key, length, block_order, block_rows)
        updated = []
        for member, member_state in zip(groups, state_now):
            advance = partial(
                attend_block,
                query_latent=member[0],
                query_rotated=member[1],
                query_place=member[2],
                key_latent=latent_block,
                key_rotated=rotated_block,
                key_place=key_place,
                score_scale=score_scale,
            )
            updated.append(advance(member_state))
        return (tuple(updated), None)

    result, unused = lax.scan(one_block, initial, (latent_blocks, rotated_blocks, block_starts))
    mixed = jnp.concatenate(
        [
            (member_state[2] / member_state[1][:, None]).astype(jnp.bfloat16)
            for member_state in result
        ],
        0,
    )
    mixed = mixed.reshape(tokens_here, heads_here, latent_width)
    output = jnp.einsum(
        "thl,lhe->the",
        mixed,
        w_value.reshape(latent_width, heads_here, VALUE_DIM),
        preferred_element_type=jnp.float32,
    )
    return output.astype(jnp.bfloat16).reshape(tokens_here, heads_here * VALUE_DIM)


def solution(mesh):
    return jax.shard_map(
        per_device,
        mesh=mesh,
        in_specs=(
            P(("group", "ctx"), "head"),
            P(("group", "ctx"), "head"),
            P(("group", "ctx"), "head"),
            P(("group", "ctx"), None),
            P(),
            P(None, "head"),
            P(None, "head"),
            P("group"),
        ),
        out_specs=P(("group", "ctx"), "head"),
        check_vma=False,
    )
```

profile of v0, /device:TPU:0, one launch (start us, length us, event | category | flops | bytes accessed | tf_op | source)
XLA Modules:
  0.0 54.3 jit_solution(1356977436039085521)
XLA Ops:
  0.0 0.0 copy-start
  0.0 0.9 %dynamic_slice.12 = f32[128]{0:T(128)S(1)} dynamic-slice(f32[512]{0:T(512)} %param.12, s32[]{:T(128)S(6)} %select_n.69), dynamic_slice_sizes={128} | dynamic-slice | bytes 1028 | tf_op jit(solution)/shard_map/dynamic_slice | solution.py:115
  0.9 0.8 %fusion.33 = f32[64]{0:T(128)S(1)} fusion(bf16[64,128]{1,0:T(8,128)(2,1)} %param.10), kind=kLoop, calls=%fused_computation.34 | loop fusion | flops 24512 | bytes 16640 | tf_op jit(solution)/shard_map/reduce_sum | solution.py:114
  1.7 8.4 %psum.7 = f32[64]{0:T(128)S(1)} all-reduce(f32[64]{0:T(128)S(1)} %fusion.33), channel_id=1, replica_groups=mesh['group'=2,'ctx'=4,'head'=4] {'head'}, use_global_device_ids=true, to_apply=%region_3.4 | all-reduce | flops 64 | bytes 512 | tf_op jit(solution)/shard_map/psum | solution.py:114
  10.1 0.8 %fusion.35 = bf16[64,128]{1,0:T(8,128)(2,1)S(1)} fusion(bf16[64,128]{1,0:T(8,128)(2,1)} %param.10, f32[128]{0:T(128)S(1)} %dynamic_slice.12, f32[64]{0:T(128)S(1)} %add_rsqrt_fusion), kind=kLoop, calls=%fused_computation.36 | loop fusion | flops 32768 | bytes 33536 | tf_op jit(solution)/shard_map/convert_element_type | solution.py:118
  10.9 5.3 %all_gather.9 = bf16[64,512]{1,0:T(8,128)(2,1)S(1)} all-gather(bf16[64,128]{1,0:T(8,128)(2,1)S(1)} %fusion.35), channel_id=1, replica_groups=mesh['group'=2,'ctx'=4,'head'=4] {'head'}, dimensions={1}, use_global_device_ids=true | all-gather | bytes 81920 | tf_op jit(solution)/shard_map/all_gather | solution.py:119
  16.2 14.1 %all_gather.10 = bf16[256,512]{1,0:T(8,128)(2,1)S(1)} all-gather(bf16[64,512]{1,0:T(8,128)(2,1)S(1)} %all_gather.9), channel_id=1, replica_groups=mesh['group'=2,'ctx'=4,'head'=4] {'ctx'}, dimensions={0}, use_global_device_ids=true | all-gather | bytes 327680 | tf_op jit(solution)/shard_map/all_gather | solution.py:121
  30.2 0.0 copy-done
  30.2 1.8 %fusion.9 = bf16[64,16,512]{2,0,1:T(8,128)(2,1)S(1)} fusion(bf16[512,2048]{1,0:T(8,128)(2,1)S(1)} %copy-done, bf16[64,2048]{1,0:T(8,128)(2,1)} %param.8), kind=kOutput, calls=%fused_computation.8 | convolution fusion | flops 134742016 | bytes 3407872 | tf_op jit(solution)/shard_map/thd,lhd->thl/dot_general | solution.py:93
  32.0 0.0 copy-start.3
  32.1 0.0 copy-start.2
  32.1 0.0 copy-start.1
  32.1 0.6 %copy.21 = bf16[64,16,512]{2,1,0:T(8,128)(2,1)S(1)} copy(bf16[64,16,512]{2,0,1:T(8,128)(2,1)S(1)} %fusion.9) | data formatting | bytes 2097152 | tf_op jit(solution)/shard_map/convert_element_type | solution.py:99
  32.7 1.5 %fusion.46 = f32[1024,256]{0,1:T(8,128)} fusion(bf16[1024,512]{1,0:T(8,128)(2,1)S(1)} %bitcast.45, bf16[256,512]{1,0:T(8,128)(2,1)S(1)} %all_gather.10), kind=kOutput, calls=%fused_computation.68 | convolution fusion | flops 268435456 | bytes 2359296 | tf_op jit(solution)/shard_map/while/body/eval_jaxpr/dot_general | solution.py:60
  34.1 0.0 copy-done.3
  34.2 0.1 select_reduce_fusion.1
  34.3 0.0 copy-done.2
  34.3 0.2 multiply_cosine_fusion
  34.5 0.1 pad_maximum_fusion
  34.6 13.3 %all_gather.11 = bf16[256,64]{1,0:T(8,128)(2,1)S(1)} all-gather(bf16[64,64]{1,0:T(8,128)(2,1)S(1)} %pad_maximum_fusion), channel_id=1, replica_groups=mesh['group'=2,'ctx'=4,'head'=4] {'ctx'}, dimensions={0}, use_global_device_ids=true | all-gather | bytes 40960 | tf_op jit(solution)/shard_map/all_gather | solution.py:122
  47.9 0.0 copy-done.1
  47.9 0.1 reshape.178
  48.0 0.2 subtract_convert_fusion
  48.2 0.1 broadcast_in_dim.74
  48.3 0.1 le.23
  48.4 0.1 select_reduce_fusion
  48.5 1.7 %fusion.45 = (f32[1024]{0:T(1024)S(1)}, f32[1024,256]{0,1:T(8,128)S(1)}) fusion(f32[1024,256]{0,1:T(8,128)} %fusion.46, bf16[256,64]{1,0:T(8,128)(2,1)S(1)} %all_gather.11, bf16[1024,32]{1,0:T(8,128)(2,1)S(1)} %bitcast.47, bf16[1024,32]{1,0:T(8,128)(2,1)S(1)} %bitcast.46, s32[1024]{0:T(1024)S(1)} %le.23, s32[256]{0:T(256)S(1)} %fusion.38), kind=kOutput, calls=%fused_computation.67 | convolution fusion | flops 35126272 | bytes 2270208 | tf_op jit(solution)/shard_map/while/body/eval_jaxpr/dot_general | solution.py:63
  50.2 0.2 fusion.21
  50.4 0.0 copy-start.4
  50.4 0.6 %divide_convert_fusion = bf16[1024,512]{1,0:T(8,128)(2,1)S(1)} fusion(bf16[256,512]{1,0:T(8,128)(2,1)S(1)} %all_gather.10, f32[1024]{0:T(1024)S(1)} %get-tuple-element.40, f32[1024]{0:T(1024)S(1)} %get-tuple-element.29, f32[1024,256]{0,1:T(8,128)S(1)} %get-tuple-element.48, f32[1024]{0:T(1024)S(1)} %broadcast_maximum_fusion, s32[1024]{0:T(1024)S(1)} %le.23, ...), kind=kOutput, calls=%fused_computation.6 | convolution fusion | flops 271056896 | bytes 2376704 | tf_op jit(solution)/shard_map/while/body/eval_jaxpr/dot_general | solution.py:71
  51.0 1.0 %copy-done.4 = bf16[512,2048]{1,0:T(8,128)(2,1)S(1)} copy-done((bf16[512,2048]{1,0:T(8,128)(2,1)S(1)}, bf16[512,2048]{1,0:T(8,128)(2,1)}, u32[]{:S(2)}) %copy-start.4) | copy-done | bytes 2097176
  52.0 1.5 %fusion.17 = bf16[16,8,8,128]{3,2,1,0:T(8,128)(2,1)S(1)} fusion(bf16[64,16,512]{2,1,0:T(8,128)(2,1)S(1)} %bitcast.48, bf16[512,2048]{1,0:T(8,128)(2,1)S(1)} %copy-done.4), kind=kOutput, calls=%fused_computation.14 | convolution fusion | flops 134348800 | bytes 3407872 | tf_op jit(solution)/shard_map/thl,lhe->the/dot_general | solution.py:157
  53.5 0.8 %copy.52 = bf16[16,8,8,128]{3,2,0,1:T(8,128)(2,1)} copy(bf16[16,8,8,128]{3,2,1,0:T(8,128)(2,1)S(1)} %fusion.17) | data formatting | bytes 524288 | tf_op jit(solution)/shard_map/reshape | solution.py:163
  (9 shorter events, 0.1 us)
Async XLA Ops:
  0.0 30.2 %copy-start = (bf16[512,2048]{1,0:T(8,128)(2,1)S(1)}, bf16[512,2048]{1,0:T(8,128)(2,1)}, u32[]{:S(2)}) copy-start(bf16[512,2048]{1,0:T(8,128)(2,1)} %param.13) | copy-start | bytes 6291460
  32.0 2.1 %copy-start.3 = (s32[8]{0:T(128)S(1)}, s32[8]{0:T(128)}, u32[]{:S(2)}) copy-start(s32[8]{0:T(128)} %param.15) | copy-start | bytes 100
  32.1 2.2 %copy-start.2 = (bf16[64,64]{1,0:T(8,128)(2,1)S(1)}, bf16[64,64]{1,0:T(8,128)(2,1)}, u32[]{:S(2)}) copy-start(bf16[64,64]{1,0:T(8,128)(2,1)} %param.11) | copy-start | bytes 24580
  32.1 15.8 %copy-start.1 = (bf16[64,1024]{1,0:T(8,128)(2,1)S(1)}, bf16[64,1024]{1,0:T(8,128)(2,1)}, u32[]{:S(2)}) copy-start(bf16[64,1024]{1,0:T(8,128)(2,1)} %param.9) | copy-start | bytes 393220
  50.4 1.6 %copy-start.4 = (bf16[512,2048]{1,0:T(8,128)(2,1)S(1)}, bf16[512,2048]{1,0:T(8,128)(2,1)}, u32[]{:S(2)}) copy-start(bf16[512,2048]{1,0:T(8,128)(2,1)} %param.14) | copy-start | bytes 6291460
where the time goes:
time: 54.7 us; the launch traced here: 54.3 us
  blocking collectives  41 us (75%)
  matrix products  7 us (13%)
  local copies, waits for them, and re-layouts  3.53 us (6%)
  other arithmetic  2.6 us (5%)
    all_gather x1, blocking collectives, per_device(): key_latent = lax.all_gather(normed, 'ctx', axis=0, tiled=True)  14.1 us
    all_gather x1, blocking collectives, per_device(): make_key_rotated = lax.all_gather(key_rotated, 'ctx', axis=0, tiled=True)  13.3 us
    psum x1, blocking collectives, per_device(): square = lax.psum(jnp.sum(column_part * column_part, axis=1), 'head')  8.37 us
    all_gather x1, blocking collectives, per_device(): normed = lax.all_gather(scaled, 'head', axis=1, tiled=True)  5.25 us
    dot_general x1, matrix products, per_device(): jnp.einsum('thd,lhd->thl', query_nope.reshape(tokens_here, heads_here, NO...  1.79 us
    dot_general x1, matrix products, attend_block(): lax.dot_general(query_rotated, key_rotated, contract, preferred_element_t...  1.65 us
    dot_general x1, matrix products, per_device(): jnp.einsum('thl,lhe->the', mixed, w_value.reshape(latent_width, heads_her...  1.49 us
    dot_general x1, matrix products, attend_block(): lax.dot_general(query_latent, key_latent, contract, preferred_element_typ...  1.46 us

commit v1 on v0

--- a/solution.py
+++ b/solution.py
@@ -10,6 +10,18 @@
 VALUE_DIM = 128
 EPSILON = 1e-06
 NEGATIVE = -1e30
+
+
+def refer_state_in(vector, group_axis="ctx"):
+    return jnp.concatenate(
+        jax.lax.all_to_all(
+            jnp.stack([vector] * jax.lax.axis_size(group_axis), axis=0),
+            axis_name=group_axis,
+            split_axis=0,
+            concat_axis=0,
+        ),
+        axis=0,
+    )
 
 
 def rope_angle(positions, width):
@@ -119,7 +131,7 @@
     normed = lax.all_gather(scaled, "head", axis=1, tiled=True)
     key_rotated = rotate_pairs(key_rope.astype(jnp.float32), query_angle).astype(jnp.bfloat16)
     key_latent = lax.all_gather(normed, "ctx", axis=0, tiled=True)
-    make_key_rotated = lax.all_gather(key_rotated, "ctx", axis=0, tiled=True)
+    make_key_rotated = refer_state_in(key_rotated)
     row_count = key_latent.shape[0]
     length = block_length(row_count, tokens_here)
     block_count = row_count // length

time: 54.7 us -> 50.5 us (0.923)
  blocking collectives: 41 us -> 25.8 us
  starting transfers between devices: 0 us -> 6.35 us
  local copies, waits for them, and re-layouts: 3.53 us -> 5.23 us
  other arithmetic: 2.6 us -> 4.1 us
  matrix products: 7 us -> 8.3 us
    all_gather x1 -> x0, blocking collectives: 13.3 us -> none  [per_device(): make_key_rotated = lax.all_gather(key_rotated, 'ctx', axis=0, tiled=True)]
    all_to_all x0 -> x1, starting transfers between devices: none -> 6.35 us  [refer_state_in(): jax.lax.all_to_all(jnp.stack([vector] * jax.lax.axis_size(group_axis), ax...]
    psum x1, blocking collectives: 8.37 us -> 6.6 us  [per_device(): square = lax.psum(jnp.sum(column_part * column_part, axis=1), 'head')]
    dot_general x1, matrix products: 1.46 us -> 2.73 us  [attend_block(): lax.dot_general(query_latent, key_latent, contract, preferred_element_typ...]
    convert_element_type x1, local copies, waits for them, and re-layouts: 0.58 us -> 1.57 us  [per_device(): absorbed.astype(jnp.bfloat16)]
    unnamed x10, local copies, waits for them, and re-layouts: 1 us -> 1.84 us
    reduce_sum x2, other arithmetic: 0.17 us -> 0.97 us  [block_positions(): jnp.sum(jnp.where(blocks[:, None] == slot_ids[None, :], table[None, :], 0...]
    convert_element_type x1, other arithmetic: 0.01 us -> 0.72 us  [per_device(): key_rope.astype(jnp.float32)]
  transfers between devices with their start and end apart: 0 -> 1, of which waited for: 0 -> 0; matrix products, arithmetic and copies ran while one was open for 0% -> 18% of each run, Pallas kernels for 0% -> 0%
where the time goes in v1:
time: 50.5 us; the launch traced here: 49.9 us
  blocking collectives  25.8 us (51%)
  matrix products  8.3 us (16%)
  starting transfers between devices  6.35 us (13%)
  local copies, waits for them, and re-layouts  5.23 us (10%)
  other arithmetic  4.1 us (8%)
    all_gather x1, blocking collectives, per_device(): key_latent = lax.all_gather(normed, 'ctx', axis=0, tiled=True)  14 us
    psum x1, blocking collectives, per_device(): square = lax.psum(jnp.sum(column_part * column_part, axis=1), 'head')  6.6 us
    all_to_all x1, starting transfers between devices, refer_state_in(): jax.lax.all_to_all(jnp.stack([vector] * jax.lax.axis_size(group_axis), ax...  6.35 us
    all_gather x1, blocking collectives, per_device(): normed = lax.all_gather(scaled, 'head', axis=1, tiled=True)  5.25 us
    dot_general x1, matrix products, attend_block(): lax.dot_general(query_latent, key_latent, contract, preferred_element_typ...  2.73 us
    unnamed x10, local copies, waits for them, and re-layouts  1.84 us
    dot_general x1, matrix products, per_device(): jnp.einsum('thd,lhd->thl', query_nope.reshape(tokens_here, heads_here, NO...  1.83 us
    dot_general x1, matrix products, attend_block(): lax.dot_general(query_rotated, key_rotated, contract, preferred_element_t...  1.65 us
  transfers between devices with their start and end apart: 1, of which 0 were waited for; matrix products, arithmetic and copies ran while one was open for 18% of the time, Pallas kernels for 0%

profile of v1, /device:TPU:0, one launch (start us, length us, event | category | flops | bytes accessed | tf_op | source)
XLA Modules:
  0.0 49.9 jit_solution(5494451421850506144)
XLA Ops:
  0.0 0.0 copy-start
  0.0 0.9 %select_reduce_fusion.1 = s32[64]{0:T(128)S(1)} fusion(s32[8]{0:T(128)} %param.15, s32[64]{0:T(128)S(1)} %and_select_fusion.1), kind=kLoop, calls=%fused_computation.43 | loop fusion | flops 1472 | bytes 544 | tf_op jit(solution)/shard_map/reduce_sum | solution.py:48
  0.9 0.7 %convert_element_type.46 = f32[64,64]{1,0:T(8,128)S(1)} convert(bf16[64,64]{1,0:T(8,128)(2,1)} %param.11) | non-fusion elementwise | flops 4096 | bytes 24576 | tf_op jit(solution)/shard_map/convert_element_type | solution.py:132
  1.7 0.2 multiply_cosine_fusion
  1.9 0.1 pad_maximum_fusion
  1.9 0.7 %reshape.184 = bf16[4,2,2048]{2,1,0:T(2,128)(2,1)} reshape(bf16[4,64,64]{2,1,0:T(8,128)(2,1)S(1)} %stack.2) | data formatting | bytes 65536
  2.7 6.3 %all-to-all-start = ((bf16[4,2,2048]{2,1,0:T(2,128)(2,1)}), bf16[4,2,2048]{2,1,0:T(2,128)(2,1)S(1)}, u32[]{:S(2)}, u32[]{:S(2)}) async-start(bf16[4,2,2048]{2,1,0:T(2,128)(2,1)} %reshape.184), calls=%async_computation | async-start | bytes 65536 | tf_op jit(solution)/shard_map/all_to_all | solution.py:17
  9.0 0.8 %fusion.33 = f32[64]{0:T(128)S(1)} fusion(bf16[64,128]{1,0:T(8,128)(2,1)} %param.10), kind=kLoop, calls=%fused_computation.34 | loop fusion | flops 24512 | bytes 16640 | tf_op jit(solution)/shard_map/reduce_sum | solution.py:126
  9.9 6.6 %psum.7 = f32[64]{0:T(128)S(1)} all-reduce(f32[64]{0:T(128)S(1)} %fusion.33), channel_id=1, replica_groups=mesh['group'=2,'ctx'=4,'head'=4] {'head'}, use_global_device_ids=true, to_apply=%region_3.4 | all-reduce | flops 64 | bytes 512 | tf_op jit(solution)/shard_map/psum | solution.py:126
  16.5 0.8 %dynamic_slice.12 = f32[128]{0:T(128)S(1)} dynamic-slice(f32[512]{0:T(512)} %param.12, s32[]{:T(128)S(6)} %select_n.69), dynamic_slice_sizes={128} | dynamic-slice | bytes 1028 | tf_op jit(solution)/shard_map/dynamic_slice | solution.py:127
  17.2 0.8 %fusion.35 = bf16[64,128]{1,0:T(8,128)(2,1)S(1)} fusion(bf16[64,128]{1,0:T(8,128)(2,1)} %param.10, f32[128]{0:T(128)S(1)} %dynamic_slice.12, f32[64]{0:T(128)S(1)} %add_rsqrt_fusion), kind=kLoop, calls=%fused_computation.36 | loop fusion | flops 32768 | bytes 33536 | tf_op jit(solution)/shard_map/convert_element_type | solution.py:130
  18.0 5.3 %all_gather.6 = bf16[64,512]{1,0:T(8,128)(2,1)S(1)} all-gather(bf16[64,128]{1,0:T(8,128)(2,1)S(1)} %fusion.35), channel_id=1, replica_groups=mesh['group'=2,'ctx'=4,'head'=4] {'head'}, dimensions={1}, use_global_device_ids=true | all-gather | bytes 81920 | tf_op jit(solution)/shard_map/all_gather | solution.py:131
  23.3 14.0 %all_gather.7 = bf16[256,512]{1,0:T(8,128)(2,1)S(1)} all-gather(bf16[64,512]{1,0:T(8,128)(2,1)S(1)} %all_gather.6), channel_id=1, replica_groups=mesh['group'=2,'ctx'=4,'head'=4] {'ctx'}, dimensions={0}, use_global_device_ids=true | all-gather | bytes 327680 | tf_op jit(solution)/shard_map/all_gather | solution.py:133
  37.2 0.0 copy-done
  37.2 0.0 copy-start.1
  37.2 1.8 %fusion.9 = bf16[64,16,512]{2,0,1:T(8,128)(2,1)S(1)} fusion(bf16[512,2048]{1,0:T(8,128)(2,1)S(1)} %copy-done, bf16[64,2048]{1,0:T(8,128)(2,1)} %param.8), kind=kOutput, calls=%fused_computation.8 | convolution fusion | flops 134742016 | bytes 3407872 | tf_op jit(solution)/shard_map/thd,lhd->thl/dot_general | solution.py:105
  39.1 0.0 copy-start.2
  39.1 1.6 %copy.21 = bf16[64,16,512]{2,1,0:T(8,128)(2,1)} copy(bf16[64,16,512]{2,0,1:T(8,128)(2,1)S(1)} %fusion.9) | data formatting | bytes 2097152 | tf_op jit(solution)/shard_map/convert_element_type | solution.py:111
  40.7 0.0 copy-done.1
  40.7 0.1 reshape.183
  40.8 0.0 copy-done.2
  40.8 0.1 select_reduce_fusion
  40.9 2.7 %fusion.46 = f32[1024,256]{0,1:T(8,128)} fusion(bf16[1024,512]{1,0:T(8,128)(2,1)} %bitcast.46, bf16[256,512]{1,0:T(8,128)(2,1)S(1)} %all_gather.7), kind=kOutput, calls=%fused_computation.68 | convolution fusion | flops 268435456 | bytes 2359296 | tf_op jit(solution)/shard_map/while/body/eval_jaxpr/dot_general | solution.py:72
  43.6 0.2 subtract_convert_fusion
  43.9 0.1 broadcast_in_dim.74
  43.9 0.1 le.23
  44.0 0.0 all-to-all-done
  44.0 0.1 reshape.185
  44.2 1.6 %fusion.45 = (f32[1024]{0:T(1024)S(1)}, f32[1024,256]{0,1:T(8,128)S(1)}) fusion(f32[1024,256]{0,1:T(8,128)} %fusion.46, bf16[256,64]{1,0:T(8,128)(2,1)S(1)} %bitcast.49, bf16[1024,32]{1,0:T(8,128)(2,1)S(1)} %bitcast.48, bf16[1024,32]{1,0:T(8,128)(2,1)S(1)} %bitcast.47, s32[1024]{0:T(1024)S(1)} %le.23, s32[256]{0:T(256)S(1)} %fusion.38), kind=kOutput, calls=%fused_computation.67 | convolution fusion | flops 35126272 | bytes 2270208 | tf_op jit(solution)/shard_map/while/body/eval_jaxpr/dot_general | solution.py:75
  45.8 0.2 fusion.21
  46.1 0.0 copy-start.3
  46.1 0.6 %divide_convert_fusion = bf16[1024,512]{1,0:T(8,128)(2,1)S(1)} fusion(bf16[256,512]{1,0:T(8,128)(2,1)S(1)} %all_gather.7, f32[1024]{0:T(1024)S(1)} %get-tuple-element.40, f32[1024]{0:T(1024)S(1)} %get-tuple-element.29, f32[1024,256]{0,1:T(8,128)S(1)} %get-tuple-element.48, f32[1024]{0:T(1024)S(1)} %broadcast_maximum_fusion, s32[1024]{0:T(1024)S(1)} %le.23, ...), kind=kOutput, calls=%fused_computation.6 | convolution fusion | flops 271056896 | bytes 2376704 | tf_op jit(solution)/shard_map/while/body/eval_jaxpr/dot_general | solution.py:83
  46.7 1.0 %copy-done.3 = bf16[512,2048]{1,0:T(8,128)(2,1)S(1)} copy-done((bf16[512,2048]{1,0:T(8,128)(2,1)S(1)}, bf16[512,2048]{1,0:T(8,128)(2,1)}, u32[]{:S(2)}) %copy-start.3) | copy-done | bytes 2097176
  47.7 1.5 %fusion.17 = bf16[16,8,8,128]{3,2,1,0:T(8,128)(2,1)S(1)} fusion(bf16[64,16,512]{2,1,0:T(8,128)(2,1)S(1)} %bitcast.50, bf16[512,2048]{1,0:T(8,128)(2,1)S(1)} %copy-done.3), kind=kOutput, calls=%fused_computation.14 | convolution fusion | flops 134348800 | bytes 3407872 | tf_op jit(solution)/shard_map/thl,lhe->the/dot_general | solution.py:169
  49.2 0.8 %copy.52 = bf16[16,8,8,128]{3,2,0,1:T(8,128)(2,1)} copy(bf16[16,8,8,128]{3,2,1,0:T(8,128)(2,1)S(1)} %fusion.17) | data formatting | bytes 524288 | tf_op jit(solution)/shard_map/reshape | solution.py:175
  (9 shorter events, 0.1 us)
Async XLA Ops:
  0.0 37.2 %copy-start = (bf16[512,2048]{1,0:T(8,128)(2,1)S(1)}, bf16[512,2048]{1,0:T(8,128)(2,1)}, u32[]{:S(2)}) copy-start(bf16[512,2048]{1,0:T(8,128)(2,1)} %param.13) | copy-start | bytes 6291460
  2.7 41.3 %all-to-all-start = ((bf16[4,2,2048]{2,1,0:T(2,128)(2,1)}), bf16[4,2,2048]{2,1,0:T(2,128)(2,1)S(1)}, u32[]{:S(2)}, u32[]{:S(2)}) async-start(bf16[4,2,2048]{2,1,0:T(2,128)(2,1)} %reshape.184), calls=%async_computation | async-start | bytes 65536 | tf_op jit(solution)/shard_map/all_to_all | solution.py:17
  37.2 3.4 %copy-start.1 = (bf16[64,1024]{1,0:T(8,128)(2,1)S(1)}, bf16[64,1024]{1,0:T(8,128)(2,1)}, u32[]{:S(2)}) copy-start(bf16[64,1024]{1,0:T(8,128)(2,1)} %param.9) | copy-start | bytes 393220
  39.1 1.7 %copy-start.2 = (s32[8]{0:T(128)S(1)}, s32[8]{0:T(128)}, u32[]{:S(2)}) copy-start(s32[8]{0:T(128)} %param.15) | copy-start | bytes 100
  46.1 1.6 %copy-start.3 = (bf16[512,2048]{1,0:T(8,128)(2,1)S(1)}, bf16[512,2048]{1,0:T(8,128)(2,1)}, u32[]{:S(2)}) copy-start(bf16[512,2048]{1,0:T(8,128)(2,1)} %param.14) | copy-start | bytes 6291460
